TPU v7x, 32 devices: a whole 2x2x4 slice. The times are simulated.
32 devices in a mesh: row: 4 (over z), col: 8 (over y, x, core).
Axes of the slice: x: 2, y: 2, z: 4, core: 2. Of those that a mesh axis runs over, the one named last changes fastest.
Arguments:
- points: float32 [16, 32768], P(None, ('row', 'col')), may hold values from -6 to 6
- inverse_scales: float32 [16], replicated, may hold values from 0.05 to 31.255105
- probe_signs: int32 [32768, 128], P(('row', 'col')), may hold values 0 or 1
Outputs:
- trace_terms: float32 [128], replicated
- logdet_terms: float32 [128], replicated
All inputs are finite; a program needn't handle non-finite values. No bound on the sum of `probe_signs` on one device may be relied on, other than what follows from the above.
Results may differ from a plain program's by a relative error of at most 0.0014.
Values may be sent and summed in bfloat16 or wider, within the bound.
A program may use at most 128 MiB of HBM per device.

v0:
```python
import math

import jax
import jax.numpy as jnp
from jax import lax
from jax.sharding import PartitionSpec as P

STEPS = 3


epsilon = 1e-06
noise_level = 1.0
jacobi_sweeps = 6


def kernel_block(left_points, right_points):
    cross_term = lax.dot_general(
        left_points,
        right_points,
        (((0,), (0,)), ((), ())),
        precision=lax.Precision.HIGHEST,
        preferred_element_type=jnp.float32,
    )
    left_norms = jnp.sum(left_points * left_points, axis=0)
    right_norms = jnp.sum(right_points * right_points, axis=0)
    distance = jnp.maximum(left_norms[:, None] + right_norms[None, :] - 2.0 * cross_term, 0.0)
    return jnp.exp(-0.5 * distance).astype(jnp.bfloat16)


def form_blocks(row_points, col_points):
    total_rows = row_points.shape[1]
    block_rows = math.gcd(total_rows, 512)
    blocked = row_points.reshape(
        row_points.shape[0], total_rows // block_rows, block_rows
    ).transpose(1, 0, 2)
    stacked = lax.map(lambda block_points: kernel_block(block_points, col_points), blocked)
    return stacked.reshape(total_rows, col_points.shape[1])


def log_weight(alpha_list, beta_list):
    degree = len(alpha_list)
    width_probes = alpha_list[0].shape[0]
    zeros_row = jnp.zeros((width_probes,), jnp.float32)
    ones_row = jnp.ones((width_probes,), jnp.float32)
    matrix = []
    vectors = []
    for first_idx in range(degree):
        entries = []
        basis_row = []
        for second_idx in range(degree):
            if first_idx == second_idx:
                entries.append(alpha_list[first_idx])
                basis_row.append(ones_row)
            elif abs(first_idx - second_idx) == 1:
                entries.append(beta_list[min(first_idx, second_idx)])
                basis_row.append(zeros_row)
            else:
                entries.append(zeros_row)
                basis_row.append(zeros_row)
        matrix.append(entries)
        vectors.append(basis_row)
    for sweep_index in range(jacobi_sweeps):
        for first_idx in range(degree):
            for second_idx in range(first_idx + 1, degree):
                coupling = matrix[first_idx][second_idx]
                rotate_by = 0.5 * jnp.arctan2(
                    2.0 * coupling, matrix[second_idx][second_idx] - matrix[first_idx][first_idx]
                )
                cosine = jnp.cos(rotate_by)
                sine_val = jnp.sin(rotate_by)
                for row_idx in range(degree):
                    left_val = matrix[row_idx][first_idx]
                    right_val = matrix[row_idx][second_idx]
                    matrix[row_idx][first_idx] = cosine * left_val - sine_val * right_val
                    matrix[row_idx][second_idx] = sine_val * left_val + cosine * right_val
                    left_vec = vectors[row_idx][first_idx]
                    right_vec = vectors[row_idx][second_idx]
                    vectors[row_idx][first_idx] = cosine * left_vec - sine_val * right_vec
                    vectors[row_idx][second_idx] = sine_val * left_vec + cosine * right_vec
                for col_idx in range(degree):
                    upper_val = matrix[first_idx][col_idx]
                    lower_val = matrix[second_idx][col_idx]
                    matrix[first_idx][col_idx] = cosine * upper_val - sine_val * lower_val
                    matrix[second_idx][col_idx] = sine_val * upper_val + cosine * lower_val
    total = zeros_row
    for index_k in range(degree):
        total = total + vectors[0][index_k] * vectors[0][index_k] * jnp.log(
            matrix[index_k][index_k]
        )
    return total


def per_device(points, inverse_scales, probe_signs):
    scaled = points * inverse_scales[:, None]
    row_points = lax.all_gather(scaled, "col", axis=1, tiled=True)
    col_points = lax.all_gather(scaled, "row", axis=1, tiled=True)
    cached = form_blocks(row_points, col_points)
    direction = 2.0 * probe_signs.astype(jnp.float32) - 1.0
    basis_prev = jnp.zeros_like(direction)
    alpha_list = []
    beta_list = []
    for lanczos_step in range(STEPS):
        squares = lax.psum(jnp.sum(direction * direction, axis=0), ("row", "col"))
        vector_half = direction.astype(jnp.bfloat16)
        gathered = lax.all_gather(vector_half, "col", axis=0, tiled=True)
        image = (
            lax.psum_scatter(
                lax.dot_general(
                    cached, gathered, (((0,), (0,)), ((), ())), preferred_element_type=jnp.float32
                ).astype(jnp.bfloat16),
                "row",
                scatter_dimension=0,
                tiled=True,
            ).astype(jnp.float32)
            + noise_level * direction
        )
        curvature = lax.psum(jnp.sum(direction * image, axis=0), ("row", "col"))
        beta_now = jnp.sqrt(squares + epsilon)
        alpha_now = curvature / (beta_now * beta_now)
        alpha_list.append(alpha_now)
        beta_list.append(beta_now)
        if lanczos_step + 1 < STEPS:
            basis_now = direction / beta_now
            direction = image / beta_now - alpha_now * basis_now - beta_now * basis_prev
            basis_prev = basis_now
    logdet_terms = log_weight(alpha_list, beta_list[1:])
    return (alpha_list[0], logdet_terms)


def solution(mesh):
    in_specs = (P(None, ("row", "col")), P(), P(("row", "col"), None))
    out_specs = (P(), P())
    return jax.shard_map(
        per_device, mesh=mesh, in_specs=in_specs, out_specs=out_specs, check_vma=False
    )
```

profile of v0, /device:TPU:0, one launch (start us, length us, event | category | flops | bytes accessed | tf_op | source)
XLA Modules:
  0.0 559.0 jit_solution(14007900071963346204)
XLA Ops:
  7.2 0.0 all-gather.4.cloned.1.call-start
  7.2 1.8 fusion.8
  9.1 0.0 reduce-scatter.4.cloned.1.call-start
  9.1 0.9 broadcast_multiply_fusion
  10.0 15.6 %all_gather.16 = f32[16,4096]{1,0:T(8,128)S(1)} all-gather(f32[16,1024]{1,0:T(8,128)S(1)} %broadcast_multiply_fusion), channel_id=1, replica_groups=mesh['row'=4,'col'=8] {'row'}, dimensions={1}, use_global_device_ids=true | all-gather | bytes 327680 | tf_op jit(solution)/shard_map/all_gather | solution.py:96
  25.7 11.0 %all_gather.15 = f32[16,8192]{1,0:T(8,128)S(1)} all-gather(f32[16,1024]{1,0:T(8,128)S(1)} %broadcast_multiply_fusion), channel_id=1, replica_groups=mesh['row'=4,'col'=8] {'col'}, dimensions={1}, use_global_device_ids=true | all-gather | bytes 589824 | tf_op jit(solution)/shard_map/all_gather | solution.py:95
  36.8 163.7 %while.12 = (s32[]{:T(128)}, bf16[16,512,4096]{2,1,0:T(8,128)(2,1)}, f32[16,16,512]{2,1,0:T(8,128)S(1)}, f32[4096]{0:T(1024)S(1)}, f32[16,4096]{1,0:T(8,128)S(1)}, /*index=5*/s32[]{:T(128)}) while((s32[]{:T(128)}, bf16[16,512,4096]{2,1,0:T(8,128)(2,1)}, f32[16,16,512]{2,1,0:T(8,128)S(1)}, f32[4096]{0:T(1024)S(1)}, f32[16,4096]{1,0:T(8,128)S(1)}, ...), condition=%wide.region_3.4_spmd, body=%wide.region_1.3_spmd.sunk | while | flops 415251968 | bytes 4543561 | solution.py:36
  36.8 10.2 %fusion.25 = bf16[16,512,4096]{2,1,0:T(8,128)(2,1)} fusion(bf16[16,512,4096]{2,1,0:T(8,128)(2,1)} %get-tuple-element.127, s32[]{:T(128)} %get-tuple-element.126, f32[16,4096]{1,0:T(8,128)S(1)} %get-tuple-element.136, f32[4096]{0:T(1024)S(1)} %get-tuple-element.135, f32[512]{0:T(512)S(1)} %fusion.24, f32[16,16,512]{2,1,0:T(8,128)S(1)} %get-tuple-element.134), kind=kOutput, calls=%fused_computation.2.clone.1 | convolution fusion | flops 415236096 | bytes 4508672 | tf_op jit(solution)/shard_map/while/body/eval_jaxpr/dot_general | solution.py:17
  47.1 10.2 %fusion.25 = bf16[16,512,4096]{2,1,0:T(8,128)(2,1)} fusion(bf16[16,512,4096]{2,1,0:T(8,128)(2,1)} %get-tuple-element.127, s32[]{:T(128)} %get-tuple-element.126, f32[16,4096]{1,0:T(8,128)S(1)} %get-tuple-element.136, f32[4096]{0:T(1024)S(1)} %get-tuple-element.135, f32[512]{0:T(512)S(1)} %fusion.24, f32[16,16,512]{2,1,0:T(8,128)S(1)} %get-tuple-element.134), kind=kOutput, calls=%fused_computation.2.clone.1 | convolution fusion | flops 415236096 | bytes 4508672 | tf_op jit(solution)/shard_map/while/body/eval_jaxpr/dot_general | solution.py:17
  57.3 10.2 %fusion.25 = bf16[16,512,4096]{2,1,0:T(8,128)(2,1)} fusion(bf16[16,512,4096]{2,1,0:T(8,128)(2,1)} %get-tuple-element.127, s32[]{:T(128)} %get-tuple-element.126, f32[16,4096]{1,0:T(8,128)S(1)} %get-tuple-element.136, f32[4096]{0:T(1024)S(1)} %get-tuple-element.135, f32[512]{0:T(512)S(1)} %fusion.24, f32[16,16,512]{2,1,0:T(8,128)S(1)} %get-tuple-element.134), kind=kOutput, calls=%fused_computation.2.clone.1 | convolution fusion | flops 415236096 | bytes 4508672 | tf_op jit(solution)/shard_map/while/body/eval_jaxpr/dot_general | solution.py:17
  67.5 10.2 %fusion.25 = bf16[16,512,4096]{2,1,0:T(8,128)(2,1)} fusion(bf16[16,512,4096]{2,1,0:T(8,128)(2,1)} %get-tuple-element.127, s32[]{:T(128)} %get-tuple-element.126, f32[16,4096]{1,0:T(8,128)S(1)} %get-tuple-element.136, f32[4096]{0:T(1024)S(1)} %get-tuple-element.135, f32[512]{0:T(512)S(1)} %fusion.24, f32[16,16,512]{2,1,0:T(8,128)S(1)} %get-tuple-element.134), kind=kOutput, calls=%fused_computation.2.clone.1 | convolution fusion | flops 415236096 | bytes 4508672 | tf_op jit(solution)/shard_map/while/body/eval_jaxpr/dot_general | solution.py:17
  77.8 10.2 %fusion.25 = bf16[16,512,4096]{2,1,0:T(8,128)(2,1)} fusion(bf16[16,512,4096]{2,1,0:T(8,128)(2,1)} %get-tuple-element.127, s32[]{:T(128)} %get-tuple-element.126, f32[16,4096]{1,0:T(8,128)S(1)} %get-tuple-element.136, f32[4096]{0:T(1024)S(1)} %get-tuple-element.135, f32[512]{0:T(512)S(1)} %fusion.24, f32[16,16,512]{2,1,0:T(8,128)S(1)} %get-tuple-element.134), kind=kOutput, calls=%fused_computation.2.clone.1 | convolution fusion | flops 415236096 | bytes 4508672 | tf_op jit(solution)/shard_map/while/body/eval_jaxpr/dot_general | solution.py:17
  88.0 10.2 %fusion.25 = bf16[16,512,4096]{2,1,0:T(8,128)(2,1)} fusion(bf16[16,512,4096]{2,1,0:T(8,128)(2,1)} %get-tuple-element.127, s32[]{:T(128)} %get-tuple-element.126, f32[16,4096]{1,0:T(8,128)S(1)} %get-tuple-element.136, f32[4096]{0:T(1024)S(1)} %get-tuple-element.135, f32[512]{0:T(512)S(1)} %fusion.24, f32[16,16,512]{2,1,0:T(8,128)S(1)} %get-tuple-element.134), kind=kOutput, calls=%fused_computation.2.clone.1 | convolution fusion | flops 415236096 | bytes 4508672 | tf_op jit(solution)/shard_map/while/body/eval_jaxpr/dot_general | solution.py:17
  98.2 10.2 %fusion.25 = bf16[16,512,4096]{2,1,0:T(8,128)(2,1)} fusion(bf16[16,512,4096]{2,1,0:T(8,128)(2,1)} %get-tuple-element.127, s32[]{:T(128)} %get-tuple-element.126, f32[16,4096]{1,0:T(8,128)S(1)} %get-tuple-element.136, f32[4096]{0:T(1024)S(1)} %get-tuple-element.135, f32[512]{0:T(512)S(1)} %fusion.24, f32[16,16,512]{2,1,0:T(8,128)S(1)} %get-tuple-element.134), kind=kOutput, calls=%fused_computation.2.clone.1 | convolution fusion | flops 415236096 | bytes 4508672 | tf_op jit(solution)/shard_map/while/body/eval_jaxpr/dot_general | solution.py:17
  108.4 10.2 %fusion.25 = bf16[16,512,4096]{2,1,0:T(8,128)(2,1)} fusion(bf16[16,512,4096]{2,1,0:T(8,128)(2,1)} %get-tuple-element.127, s32[]{:T(128)} %get-tuple-element.126, f32[16,4096]{1,0:T(8,128)S(1)} %get-tuple-element.136, f32[4096]{0:T(1024)S(1)} %get-tuple-element.135, f32[512]{0:T(512)S(1)} %fusion.24, f32[16,16,512]{2,1,0:T(8,128)S(1)} %get-tuple-element.134), kind=kOutput, calls=%fused_computation.2.clone.1 | convolution fusion | flops 415236096 | bytes 4508672 | tf_op jit(solution)/shard_map/while/body/eval_jaxpr/dot_general | solution.py:17
  118.6 10.3 %fusion.25 = bf16[16,512,4096]{2,1,0:T(8,128)(2,1)} fusion(bf16[16,512,4096]{2,1,0:T(8,128)(2,1)} %get-tuple-element.127, s32[]{:T(128)} %get-tuple-element.126, f32[16,4096]{1,0:T(8,128)S(1)} %get-tuple-element.136, f32[4096]{0:T(1024)S(1)} %get-tuple-element.135, f32[512]{0:T(512)S(1)} %fusion.24, f32[16,16,512]{2,1,0:T(8,128)S(1)} %get-tuple-element.134), kind=kOutput, calls=%fused_computation.2.clone.1 | convolution fusion | flops 415236096 | bytes 4508672 | tf_op jit(solution)/shard_map/while/body/eval_jaxpr/dot_general | solution.py:17
  128.9 10.2 %fusion.25 = bf16[16,512,4096]{2,1,0:T(8,128)(2,1)} fusion(bf16[16,512,4096]{2,1,0:T(8,128)(2,1)} %get-tuple-element.127, s32[]{:T(128)} %get-tuple-element.126, f32[16,4096]{1,0:T(8,128)S(1)} %get-tuple-element.136, f32[4096]{0:T(1024)S(1)} %get-tuple-element.135, f32[512]{0:T(512)S(1)} %fusion.24, f32[16,16,512]{2,1,0:T(8,128)S(1)} %get-tuple-element.134), kind=kOutput, calls=%fused_computation.2.clone.1 | convolution fusion | flops 415236096 | bytes 4508672 | tf_op jit(solution)/shard_map/while/body/eval_jaxpr/dot_general | solution.py:17
  139.2 10.2 %fusion.25 = bf16[16,512,4096]{2,1,0:T(8,128)(2,1)} fusion(bf16[16,512,4096]{2,1,0:T(8,128)(2,1)} %get-tuple-element.127, s32[]{:T(128)} %get-tuple-element.126, f32[16,4096]{1,0:T(8,128)S(1)} %get-tuple-element.136, f32[4096]{0:T(1024)S(1)} %get-tuple-element.135, f32[512]{0:T(512)S(1)} %fusion.24, f32[16,16,512]{2,1,0:T(8,128)S(1)} %get-tuple-element.134), kind=kOutput, calls=%fused_computation.2.clone.1 | convolution fusion | flops 415236096 | bytes 4508672 | tf_op jit(solution)/shard_map/while/body/eval_jaxpr/dot_general | solution.py:17
  149.4 10.2 %fusion.25 = bf16[16,512,4096]{2,1,0:T(8,128)(2,1)} fusion(bf16[16,512,4096]{2,1,0:T(8,128)(2,1)} %get-tuple-element.127, s32[]{:T(128)} %get-tuple-element.126, f32[16,4096]{1,0:T(8,128)S(1)} %get-tuple-element.136, f32[4096]{0:T(1024)S(1)} %get-tuple-element.135, f32[512]{0:T(512)S(1)} %fusion.24, f32[16,16,512]{2,1,0:T(8,128)S(1)} %get-tuple-element.134), kind=kOutput, calls=%fused_computation.2.clone.1 | convolution fusion | flops 415236096 | bytes 4508672 | tf_op jit(solution)/shard_map/while/body/eval_jaxpr/dot_general | solution.py:17
  159.6 10.3 %fusion.25 = bf16[16,512,4096]{2,1,0:T(8,128)(2,1)} fusion(bf16[16,512,4096]{2,1,0:T(8,128)(2,1)} %get-tuple-element.127, s32[]{:T(128)} %get-tuple-element.126, f32[16,4096]{1,0:T(8,128)S(1)} %get-tuple-element.136, f32[4096]{0:T(1024)S(1)} %get-tuple-element.135, f32[512]{0:T(512)S(1)} %fusion.24, f32[16,16,512]{2,1,0:T(8,128)S(1)} %get-tuple-element.134), kind=kOutput, calls=%fused_computation.2.clone.1 | convolution fusion | flops 415236096 | bytes 4508672 | tf_op jit(solution)/shard_map/while/body/eval_jaxpr/dot_general | solution.py:17
  169.9 10.2 %fusion.25 = bf16[16,512,4096]{2,1,0:T(8,128)(2,1)} fusion(bf16[16,512,4096]{2,1,0:T(8,128)(2,1)} %get-tuple-element.127, s32[]{:T(128)} %get-tuple-element.126, f32[16,4096]{1,0:T(8,128)S(1)} %get-tuple-element.136, f32[4096]{0:T(1024)S(1)} %get-tuple-element.135, f32[512]{0:T(512)S(1)} %fusion.24, f32[16,16,512]{2,1,0:T(8,128)S(1)} %get-tuple-element.134), kind=kOutput, calls=%fused_computation.2.clone.1 | convolution fusion | flops 415236096 | bytes 4508672 | tf_op jit(solution)/shard_map/while/body/eval_jaxpr/dot_general | solution.py:17
  180.1 10.2 %fusion.25 = bf16[16,512,4096]{2,1,0:T(8,128)(2,1)} fusion(bf16[16,512,4096]{2,1,0:T(8,128)(2,1)} %get-tuple-element.127, s32[]{:T(128)} %get-tuple-element.126, f32[16,4096]{1,0:T(8,128)S(1)} %get-tuple-element.136, f32[4096]{0:T(1024)S(1)} %get-tuple-element.135, f32[512]{0:T(512)S(1)} %fusion.24, f32[16,16,512]{2,1,0:T(8,128)S(1)} %get-tuple-element.134), kind=kOutput, calls=%fused_computation.2.clone.1 | convolution fusion | flops 415236096 | bytes 4508672 | tf_op jit(solution)/shard_map/while/body/eval_jaxpr/dot_general | solution.py:17
  190.3 10.2 %fusion.25 = bf16[16,512,4096]{2,1,0:T(8,128)(2,1)} fusion(bf16[16,512,4096]{2,1,0:T(8,128)(2,1)} %get-tuple-element.127, s32[]{:T(128)} %get-tuple-element.126, f32[16,4096]{1,0:T(8,128)S(1)} %get-tuple-element.136, f32[4096]{0:T(1024)S(1)} %get-tuple-element.135, f32[512]{0:T(512)S(1)} %fusion.24, f32[16,16,512]{2,1,0:T(8,128)S(1)} %get-tuple-element.134), kind=kOutput, calls=%fused_computation.2.clone.1 | convolution fusion | flops 415236096 | bytes 4508672 | tf_op jit(solution)/shard_map/while/body/eval_jaxpr/dot_general | solution.py:17
  200.5 29.2 %convolution_convert_fusion.2 = bf16[4096,128]{1,0:T(8,128)(2,1)} fusion(bf16[8192,4096]{1,0:T(8,128)(2,1)} %bitcast.3, bf16[8192,128]{1,0:T(8,128)(2,1)} %all-gather.4.cloned.1.call-done), kind=kOutput, calls=%fused_computation.10 | convolution fusion | flops 8590458880 | bytes 70254592 | tf_op jit(solution)/shard_map/dot_general | solution.py:108
  229.7 0.0 reduce-scatter.4.cloned.1.call-update
  229.7 0.0 all-gather.6.cloned.1.call-start
  229.7 28.3 %reduce-scatter.4.cloned.1.call-done = bf16[1024,128]{1,0:T(8,128)(2,1)} async-done(((bf16[4096,128]{1,0:T(8,128)(2,1)}), bf16[1024,128]{1,0:T(8,128)(2,1)}) %reduce-scatter.4.cloned.1.call-update) | async-done | bytes 262160 | tf_op jit(solution)/shard_map/reduce_scatter | solution.py:107
  258.1 1.1 multiply_reduce_fusion.3
  259.2 38.9 %all-reduce.2 = (f32[128]{0:T(128)S(1)}, f32[128]{0:T(128)S(1)}) all-reduce(f32[128]{0:T(128)S(1)} %get-tuple-element.63, f32[128]{0:T(128)S(1)} %get-tuple-element.62), channel_id=1, replica_groups=mesh['row'=4,'col'=8] {'row','col'}, use_global_device_ids=true, to_apply=%region_6.7 | all-reduce | flops 256 | bytes 2048 | tf_op jit(solution)/shard_map/psum | solution.py:117
  298.1 1.9 fusion.10
  299.9 0.0 all-gather.6.cloned.1.call-update
  300.0 0.0 reduce-scatter.6.cloned.1.call-start
  300.0 27.6 %all-gather.6.cloned.1.call-done = bf16[8192,128]{1,0:T(8,128)(2,1)} async-done(((bf16[1024,128]{1,0:T(8,128)(2,1)}), bf16[8192,128]{1,0:T(8,128)(2,1)}) %all-gather.6.cloned.1.call-update) | async-done | bytes 2097168 | tf_op jit(solution)/shard_map/all_gather | solution.py:105
  327.6 29.1 %convolution_convert_fusion.1 = bf16[4096,128]{1,0:T(8,128)(2,1)} fusion(bf16[8192,4096]{1,0:T(8,128)(2,1)} %bitcast.3, bf16[8192,128]{1,0:T(8,128)(2,1)} %all-gather.6.cloned.1.call-done), kind=kOutput, calls=%fused_computation.9 | convolution fusion | flops 8590458880 | bytes 70254592 | tf_op jit(solution)/shard_map/dot_general | solution.py:108
  356.8 0.0 reduce-scatter.6.cloned.1.call-update
  356.8 0.0 all-gather.8.cloned.1.call-start
  356.8 27.4 %reduce-scatter.6.cloned.1.call-done = bf16[1024,128]{1,0:T(8,128)(2,1)} async-done(((bf16[4096,128]{1,0:T(8,128)(2,1)}), bf16[1024,128]{1,0:T(8,128)(2,1)}) %reduce-scatter.6.cloned.1.call-update) | async-done | bytes 262160 | tf_op jit(solution)/shard_map/reduce_scatter | solution.py:107
  384.2 1.1 multiply_reduce_fusion.2
  385.3 38.7 %all-reduce.1 = (f32[128]{0:T(128)S(1)}, f32[128]{0:T(128)S(1)}) all-reduce(f32[128]{0:T(128)S(1)} %get-tuple-element.61, f32[128]{0:T(128)S(1)} %get-tuple-element.60), channel_id=1, replica_groups=mesh['row'=4,'col'=8] {'row','col'}, use_global_device_ids=true, to_apply=%region_13.14 | all-reduce | flops 256 | bytes 2048 | tf_op jit(solution)/shard_map/psum | solution.py:117
  424.1 1.9 fusion.9
  426.0 0.0 all-gather.8.cloned.1.call-update
  426.0 0.3 reduce-scatter.8.cloned.1.call-start
  426.3 27.4 %all-gather.8.cloned.1.call-done = bf16[8192,128]{1,0:T(8,128)(2,1)} async-done(((bf16[1024,128]{1,0:T(8,128)(2,1)}), bf16[8192,128]{1,0:T(8,128)(2,1)}) %all-gather.8.cloned.1.call-update) | async-done | bytes 2097168 | tf_op jit(solution)/shard_map/all_gather | solution.py:105
  453.7 29.1 %convolution_convert_fusion = bf16[4096,128]{1,0:T(8,128)(2,1)} fusion(bf16[8192,4096]{1,0:T(8,128)(2,1)} %bitcast.3, bf16[8192,128]{1,0:T(8,128)(2,1)} %all-gather.8.cloned.1.call-done), kind=kOutput, calls=%fused_computation.8 | convolution fusion | flops 8590458880 | bytes 70254592 | tf_op jit(solution)/shard_map/dot_general | solution.py:108
  482.8 27.4 %reduce-scatter.8.cloned.1.call-done = bf16[1024,128]{1,0:T(8,128)(2,1)} async-done(((bf16[4096,128]{1,0:T(8,128)(2,1)}), bf16[1024,128]{1,0:T(8,128)(2,1)}) %reduce-scatter.8.cloned.1.call-update) | async-done | bytes 262160 | tf_op jit(solution)/shard_map/reduce_scatter | solution.py:107
  510.3 1.1 multiply_reduce_fusion
  511.4 38.7 %all-reduce = (f32[128]{0:T(128)S(1)}, f32[128]{0:T(128)S(1)}) all-reduce(f32[128]{0:T(128)S(1)} %get-tuple-element.59, f32[128]{0:T(128)S(1)} %get-tuple-element.58), channel_id=1, replica_groups=mesh['row'=4,'col'=8] {'row','col'}, use_global_device_ids=true, to_apply=%region_18.19 | all-reduce | flops 256 | bytes 2048 | tf_op jit(solution)/shard_map/psum | solution.py:117
  550.1 2.0 multiply_add_fusion.1
  (28 shorter events, 0.5 us)
Async XLA Ops:
  7.2 193.3 %all-gather.4.cloned.1.call-start = ((), (), s32[]{:S(2)}) async-start(), calls=%async_computation.3 | async-start | bytes 2359296 | tf_op jit(solution)/shard_map/all_gather | solution.py:105
  9.1 249.0 %reduce-scatter.4.cloned.1.call-start = ((), (), s32[]{:S(2)}) async-start(), calls=%async_computation.4 | async-start | bytes 1310720 | tf_op jit(solution)/shard_map/reduce_scatter | solution.py:107
  200.5 57.5 %copy-start = (s32[1024,128]{1,0:T(8,128)S(1)}, s32[1024,128]{1,0:T(8,128)}, u32[]{:S(2)}) copy-start(s32[1024,128]{1,0:T(8,128)} %param.7) | copy-start | bytes 1572868
  229.7 98.0 %all-gather.6.cloned.1.call-start = ((), (), s32[]{:S(2)}) async-start(), calls=%async_computation.5 | async-start | bytes 2359296 | tf_op jit(solution)/shard_map/all_gather | solution.py:105
  298.1 252.0 %copy-start.1 = (f32[128]{0:T(128)}, f32[128]{0:T(128)S(1)}, u32[]{:S(2)}) copy-start(f32[128]{0:T(128)S(1)} %get-tuple-element.87) | copy-start | bytes 1540
  300.0 84.3 %reduce-scatter.6.cloned.1.call-start = ((), (), s32[]{:S(2)}) async-start(), calls=%async_computation.6 | async-start | bytes 1310720 | tf_op jit(solution)/shard_map/reduce_scatter | solution.py:107
  356.8 96.9 %all-gather.8.cloned.1.call-start = ((), (), s32[]{:S(2)}) async-start(), calls=%async_computation.7 | async-start | bytes 2359296 | tf_op jit(solution)/shard_map/all_gather | solution.py:105
  426.0 84.3 %reduce-scatter.8.cloned.1.call-start = ((), (), s32[]{:S(2)}) async-start(), calls=%async_computation.8 | async-start | bytes 1310720 | tf_op jit(solution)/shard_map/reduce_scatter | solution.py:107
Sparse Core Ops, SparseCore 0:
  9.9 31.1 all-gather.3
  229.8 28.1 reduce-scatter.3
  300.1 27.5 all-gather.5
  356.9 27.2 reduce-scatter.5
  426.1 27.5 all-gather.7
  482.9 27.2 reduce-scatter.7
where the time goes:
time: 560 us; the launch traced here: 559 us
  matrix products  251 us (45%)
  blocking collectives  143 us (26%)
  waiting for transfers between devices  138 us (25%)
  between operations  14.1 us (3%)
  other arithmetic  12.3 us (2%)
    dot_general x16, matrix products, kernel_block(): lax.dot_general(left_points, right_points, (((0,), (0,)), ((), ())), prec...  163 us
    psum x3, blocking collectives, per_device(): curvature = lax.psum(jnp.sum(direction * image, axis=0), ('row', 'col'))  116 us
    dot_general x3, matrix products, per_device(): lax.dot_general(cached, gathered, (((0,), (0,)), ((), ())), preferred_ele...  87.4 us
    reduce_scatter x3, waiting for transfers between devices, per_device(): lax.psum_scatter(lax.dot_general(cached, gathered, (((0,), (0,)), ((), ()...  83.2 us
    all_gather x3, waiting for transfers between devices, per_device(): gathered = lax.all_gather(vector_half, 'col', axis=0, tiled=True)  55.1 us
    all_gather x1, blocking collectives, per_device(): col_points = lax.all_gather(scaled, 'row', axis=1, tiled=True)  15.6 us
  transfers between devices with their start and end apart: 6, of which 5 were waited for; matrix products, arithmetic and copies ran while one was open for 29% of the time, Pallas kernels for 0%

commit v1 on v0

v1 whole, which is shorter than its diff:
```python
import functools
import math

import jax
import jax.numpy as jnp
from jax import lax
from jax.experimental import pallas as pl
from jax.experimental.pallas import tpu as pltpu
from jax.sharding import PartitionSpec as P

STEPS = 3


epsilon = 1e-06
noise_level = 1.0
jacobi_sweeps = 6
MESH = pl.DeviceIdType.MESH


def flip(index, mask):
    bit = 1
    out = index
    while bit <= mask:
        if mask & bit:
            out = out + bit * (1 - 2 * ((index // bit) % 2))
        bit *= 2
    return out


def relay_bit(row_off, col_off):
    bits = [1 << k for k in range(1, 16) if col_off & (1 << k)]
    return bits[0] if row_off % 2 == 0 else bits[-1]


def plan(rows, cols):
    def key(off):
        row_off, col_off = off
        odd = col_off & 1
        depth = bin(col_off >> 1).count("1")
        when = (0.0, 8.0, 12.0, 16.0, 20.0)[depth]
        return (row_off * 10 + when + odd * (1.0 if depth != 1 else 1.5), row_off, col_off)

    order = sorted(((r, c) for r in range(rows) for c in range(cols)), key=key)
    where = {off: k for k, off in enumerate(order)}
    children = []
    for row_off, col_off in order:
        mine = []
        if col_off % 2 == 0:
            bit = 2
            while bit < cols:
                target = col_off | bit
                if not col_off & bit and relay_bit(row_off, target) == bit:
                    mine.append((0, bit, where[(row_off, target)]))
                bit *= 2
            if row_off == 0 and col_off == 0:
                for other in range(1, rows):
                    mine.append((other, 0, where[(other, 0)]))
            if cols > 1:
                mine.append((0, 1, where[(row_off, col_off + 1)]))
        children.append(mine)
    return order, children


def three_parts(x):
    high = x.astype(jnp.bfloat16).astype(jnp.float32)
    rest = x - high
    middle = rest.astype(jnp.bfloat16).astype(jnp.float32)
    low = (rest - middle).astype(jnp.bfloat16).astype(jnp.float32)
    return high, middle, low


def features(x, left):
    high, middle, low = three_parts(x)
    norm = -0.5 * jnp.sum(x * x, axis=0, keepdims=True)
    parts = three_parts(norm)
    rows = lax.broadcasted_iota(jnp.int32, x.shape, 0)
    first = 0 if left else 3
    ones_at = 3 if left else 0
    tail = jnp.where((rows >= ones_at) & (rows < ones_at + 3), 1.0, 0.0)
    for k in range(3):
        tail = jnp.where(rows == first + k, parts[k], tail)
    blank = jnp.zeros_like(x)
    if left:
        groups = [high, high, middle, middle, high, low, tail, blank]
    else:
        groups = [high, middle, high, middle, low, high, tail, blank]
    return jnp.concatenate(groups, axis=0)


def tree_sum(values):
    while len(values) > 1:
        values = [values[k] + values[k + 1] for k in range(0, len(values), 2)]
    return values[0]


def kernel(
    rows, cols, order, children,
    pts_ref, signs_ref,
    sums_ref, far_ref,
    near, stage, vecs, points, left, right, total, direction, before,
    sums_out, sums_mid, sums_col, sums_row,
    pts_recv, pts_send, vec_recv, vec_send, write_sem, read_sem,
    col_recv, col_send, row_recv, row_send,
):
    blocks = rows * cols
    half = blocks // 2
    n = pts_ref.shape[1]
    probes = signs_ref.shape[0]
    my_row, my_col = lax.axis_index("row"), lax.axis_index("col")

    def device(row_off, col_off):
        return (flip(my_row, row_off), flip(my_col, col_off))

    copies = [(k, child) for k in range(blocks) for child in children[k]]
    number = {(k, child): i for i, (k, child) in enumerate(copies)}

    def remote(buffer, own, recv, send, k, child):
        row_off, col_off, target = child
        return pltpu.make_async_remote_copy(
            src_ref=own if k == 0 else buffer.at[k],
            dst_ref=buffer.at[target],
            send_sem=send.at[number[(k, child)]],
            recv_sem=recv.at[target],
            device_id=device(row_off, col_off),
            device_id_type=MESH,
        )

    def arrived(buffer, own, recv, send, k):
        if k:
            pltpu.make_async_remote_copy(
                src_ref=buffer.at[k],
                dst_ref=buffer.at[k],
                send_sem=send.at[0],
                recv_sem=recv.at[k],
                device_id=device(0, 1),
                device_id_type=MESH,
            ).wait_recv()
        for child in children[k]:
            remote(buffer, own, recv, send, k, child).start()

    def sent(buffer, own, recv, send):
        for k, child in copies:
            remote(buffer, own, recv, send, k, child).wait_send()

    barrier = pltpu.get_barrier_semaphore()
    peers = [(0, c) for c in range(1, cols)] + [(r, 0) for r in range(1, rows)]
    for peer in peers:
        pl.semaphore_signal(barrier, inc=1, device_id=device(*peer), device_id_type=MESH)
    pl.semaphore_wait(barrier, len(peers))

    pts = (points, pts_ref, pts_recv, pts_send)
    arrived(*pts, 0)
    points[0] = pts_ref[...]
    vecs[0] = signs_ref[...]
    direction[...] = signs_ref[...].astype(jnp.float32)
    right[...] = features(pts_ref[...], False).astype(jnp.bfloat16)
    for k in range(1, blocks):
        arrived(*pts, k)

    def poll(pack, pair):
        group = max(half // 4, 1)
        for g in range(0, half, group):
            @pl.when((pair >= g) & (pair < g + group))
            def _():
                for t in range(g, min(g + group, half)):
                    @pl.when(pair == t)
                    def _():
                        for k in (2 * t, 2 * t + 1):
                            arrived(*pack, k)

    def form(k, chunk):
        left[...] = features(points[k], True).T.astype(jnp.bfloat16)
        tile = math.gcd(n, 256)

        def body(j, carry):
            part = pl.ds(pl.multiple_of(j * tile, tile), tile)
            power = jnp.dot(left[part, :], right[...], preferred_element_type=jnp.float32)
            chunk[part, :] = jnp.exp2(jnp.minimum(power, 0.0)).astype(jnp.bfloat16)
            return carry

        lax.fori_loop(0, n // tile, body, 0)

    def apply(k, chunk):
        total[...] += jnp.dot(vecs[k], chunk[...], preferred_element_type=jnp.float32)

    def write(slot, pair):
        return pltpu.make_async_copy(stage.at[slot], far_ref.at[pair], write_sem.at[slot])

    def read(slot, pair):
        return pltpu.make_async_copy(far_ref.at[pair], stage.at[slot], read_sem.at[slot])

    def column_sums(x):
        width = math.gcd(n, 128)
        folded = sum(x[:, s : s + width] for s in range(0, n, width))
        return jnp.sum(folded.T, axis=0, keepdims=True)

    def exchange(step, squares, curvature):
        sums_out[step] = jnp.concatenate(
            [squares, curvature, jnp.zeros((6, probes), jnp.float32)], axis=0
        )
        for source, target, recv, send, count, across in (
            (sums_out, sums_col, col_recv, col_send, cols, False),
            (sums_mid, sums_row, row_recv, row_send, rows, True),
        ):
            moves = [
                pltpu.make_async_remote_copy(
                    src_ref=source.at[step],
                    dst_ref=target.at[step, off],
                    send_sem=send.at[step, off],
                    recv_sem=recv.at[step, off],
                    device_id=device(off, 0) if across else device(0, off),
                    device_id_type=MESH,
                )
                for off in range(1, count)
            ]
            for move in moves:
                move.start()
            for move in moves:
                move.wait()
            result = tree_sum(
                [source[step]] + [target[step, off] for off in range(1, count)]
            )
            if not across:
                sums_mid[step] = result
        return result

    def spread(row):
        return jnp.broadcast_to(row, (probes, probes)).T

    for step in range(STEPS):
        total[...] = jnp.zeros_like(total)
        pack = (vecs, signs_ref if step == 0 else vecs.at[0], vec_recv, vec_send)
        if step == 0:
            def first(pair, carry):
                poll(pack, pair)
                slot = lax.rem(pair, 2)
                form(2 * pair, near.at[pair])
                apply(2 * pair, near.at[pair])

                @pl.when(pair >= 2)
                def _():
                    write(slot, pair - 2).wait()

                form(2 * pair + 1, stage.at[slot])
                write(slot, pair).start()
                apply(2 * pair + 1, stage.at[slot])
                return carry

            lax.fori_loop(0, half, first, 0)
            for pair in range(max(half - 2, 0), half):
                write(pair % 2, pair).wait()
        else:
            def later(pair, carry):
                poll(pack, pair)
                slot = lax.rem(pair, 2)

                @pl.when(pair + 1 < half)
                def _():
                    read(1 - slot, pair + 1).start()

                apply(2 * pair, near.at[pair])
                read(slot, pair).wait()
                apply(2 * pair + 1, stage.at[slot])
                return carry

            read(0, 0).start()
            lax.fori_loop(0, half, later, 0)
        sent(*pack)
        if step == 0:
            sent(*pts)
        now = direction[...]
        image = total[...] + noise_level * now
        result = exchange(step, column_sums(now * now), column_sums(now * image))
        squares, curvature = result[0:1], result[1:2]
        sums_ref[step] = result
        if step + 1 < STEPS:
            beta = jnp.sqrt(squares + epsilon)
            alpha = curvature / (beta * beta)
            inverse = spread(1.0 / beta)
            alpha_all, beta_all = spread(alpha), spread(beta)
            for s in range(0, n, 128):
                part = slice(s, s + 128)
                basis = direction[:, part] * inverse
                fresh = (total[:, part] + noise_level * direction[:, part]) * inverse - alpha_all * basis
                if step > 0:
                    fresh = fresh - beta_all * before[:, part]
                before[:, part] = basis
                direction[:, part] = fresh
                vecs[0, :, part] = fresh.astype(jnp.bfloat16)


def log_weight(alpha_list, beta_list):
    degree = len(alpha_list)
    width_probes = alpha_list[0].shape[0]
    zeros_row = jnp.zeros((width_probes,), jnp.float32)
    ones_row = jnp.ones((width_probes,), jnp.float32)
    matrix = []
    vectors = []
    for first_idx in range(degree):
        entries = []
        basis_row = []
        for second_idx in range(degree):
            if first_idx == second_idx:
                entries.append(alpha_list[first_idx])
                basis_row.append(ones_row)
            elif abs(first_idx - second_idx) == 1:
                entries.append(beta_list[min(first_idx, second_idx)])
                basis_row.append(zeros_row)
            else:
                entries.append(zeros_row)
                basis_row.append(zeros_row)
        matrix.append(entries)
        vectors.append(basis_row)
    for sweep_index in range(jacobi_sweeps):
        for first_idx in range(degree):
            for second_idx in range(first_idx + 1, degree):
                coupling = matrix[first_idx][second_idx]
                rotate_by = 0.5 * jnp.arctan2(
                    2.0 * coupling, matrix[second_idx][second_idx] - matrix[first_idx][first_idx]
                )
                cosine = jnp.cos(rotate_by)
                sine_val = jnp.sin(rotate_by)
                for row_idx in range(degree):
                    left_val = matrix[row_idx][first_idx]
                    right_val = matrix[row_idx][second_idx]
                    matrix[row_idx][first_idx] = cosine * left_val - sine_val * right_val
                    matrix[row_idx][second_idx] = sine_val * left_val + cosine * right_val
                    left_vec = vectors[row_idx][first_idx]
                    right_vec = vectors[row_idx][second_idx]
                    vectors[row_idx][first_idx] = cosine * left_vec - sine_val * right_vec
                    vectors[row_idx][second_idx] = sine_val * left_vec + cosine * right_vec
                for col_idx in range(degree):
                    upper_val = matrix[first_idx][col_idx]
                    lower_val = matrix[second_idx][col_idx]
                    matrix[first_idx][col_idx] = cosine * upper_val - sine_val * lower_val
                    matrix[second_idx][col_idx] = sine_val * upper_val + cosine * lower_val
    total = zeros_row
    for index_k in range(degree):
        total = total + vectors[0][index_k] * vectors[0][index_k] * jnp.log(
            matrix[index_k][index_k]
        )
    return total


def per_device(rows, cols, points, inverse_scales, probe_signs):
    dims, n = points.shape
    probes = probe_signs.shape[1]
    blocks = rows * cols
    half = blocks // 2
    order, children = plan(rows, cols)
    copies = sum(len(c) for c in children)
    scaled = points * inverse_scales[:, None] * math.sqrt(math.log2(math.e))
    signs = (2.0 * probe_signs.astype(jnp.float32) - 1.0).T.astype(jnp.bfloat16)
    dma = pltpu.SemaphoreType.DMA
    vmem = pltpu.VMEM
    sums, _ = pl.pallas_call(
        functools.partial(kernel, rows, cols, order, children),
        out_shape=(
            jax.ShapeDtypeStruct((STEPS, 8, probes), jnp.float32),
            jax.ShapeDtypeStruct((half, n, n), jnp.bfloat16),
        ),
        in_specs=[pl.BlockSpec(memory_space=pltpu.VMEM)] * 2,
        out_specs=(
            pl.BlockSpec(memory_space=pltpu.VMEM),
            pl.BlockSpec(memory_space=pl.ANY),
        ),
        scratch_shapes=[
            vmem((half, n, n), jnp.bfloat16),
            vmem((2, n, n), jnp.bfloat16),
            vmem((blocks, probes, n), jnp.bfloat16),
            vmem((blocks, dims, n), jnp.float32),
            vmem((n, 8 * dims), jnp.bfloat16),
            vmem((8 * dims, n), jnp.bfloat16),
            vmem((probes, n), jnp.float32),
            vmem((probes, n), jnp.float32),
            vmem((probes, n), jnp.float32),
            vmem((STEPS, 8, probes), jnp.float32),
            vmem((STEPS, 8, probes), jnp.float32),
            vmem((STEPS, cols, 8, probes), jnp.float32),
            vmem((STEPS, rows, 8, probes), jnp.float32),
            dma((blocks,)),
            dma((copies,)),
            dma((blocks,)),
            dma((copies,)),
            dma((2,)),
            dma((2,)),
            dma((STEPS, cols)),
            dma((STEPS, cols)),
            dma((STEPS, rows)),
            dma((STEPS, rows)),
        ],
        compiler_params=pltpu.CompilerParams(
            collective_id=0, has_side_effects=True, vmem_limit_bytes=64 * 2**20 - 65536
        ),
        name="lanczos",
    )(scaled, signs)
    beta_list = [jnp.sqrt(sums[k, 0] + epsilon) for k in range(STEPS)]
    alpha_list = [sums[k, 1] / (beta_list[k] * beta_list[k]) for k in range(STEPS)]
    return alpha_list[0], log_weight(alpha_list, beta_list[1:])


def solution(mesh):
    in_specs = (P(None, ("row", "col")), P(), P(("row", "col"), None))
    out_specs = (P(), P())
    return jax.shard_map(
        functools.partial(per_device, mesh.shape["row"], mesh.shape["col"]),
        mesh=mesh, in_specs=in_specs, out_specs=out_specs, check_vma=False,
    )
```

time: 560 us -> 231 us (0.41)
  matrix products: 251 us -> 0 us
  Pallas kernels: 0 us -> 224 us
  blocking collectives: 143 us -> 0 us
  waiting for transfers between devices: 138 us -> 0 us
  between operations: 14.1 us -> 0.65 us
  other arithmetic: 12.3 us -> 5.13 us
    dot_general x19 -> x0, matrix products: 251 us -> none  [the longest x16 163 us: kernel_block(): lax.dot_general(left_points, right_points, (((0,), (0,)), ((), ())), prec...]
    pallas_call x0 -> x1, Pallas kernels: none -> 224 us  [per_device(): pl.pallas_call(functools.partial(kernel, rows, cols, order, children), ou...]
    psum x3 -> x0, blocking collectives: 116 us -> none  [per_device(): curvature = lax.psum(jnp.sum(direction * image, axis=0), ('row', 'col'))]
    reduce_scatter x3 -> x0, waiting for transfers between devices: 83.2 us -> none  [per_device(): lax.psum_scatter(lax.dot_general(cached, gathered, (((0,), (0,)), ((), ()...]
    all_gather x3 -> x0, waiting for transfers between devices: 55.1 us -> none  [per_device(): gathered = lax.all_gather(vector_half, 'col', axis=0, tiled=True)]
    all_gather x2 -> x0, blocking collectives: 26.7 us -> none  [the longest x1 15.6 us: per_device(): col_points = lax.all_gather(scaled, 'row', axis=1, tiled=True)]
  transfers between devices with their start and end apart: 6 -> 0, of which waited for: 5 -> 0; matrix products, arithmetic and copies ran while one was open for 29% -> 0% of each run, Pallas kernels for 0% -> 0%
where the time goes in v1:
time: 231 us
  Pallas kernels  224 us (97%)
  other arithmetic  5.13 us (2%)
    pallas_call x1, Pallas kernels, per_device(): pl.pallas_call(functools.partial(kernel, rows, cols, order, children), ou...  224 us

profile of v1, /device:TPU:0, one launch (start us, length us, event | category | flops | bytes accessed | tf_op | source)
XLA Modules:
  0.0 230.7 jit_solution(18008572986152802729)
XLA Ops:
  0.6 1.5 multiply_multiply_fusion.pts_ref
  2.2 1.2 copy.5
  3.4 0.8 fusion.signs_ref
  4.2 223.6 %lanczos.1 = (f32[3,8,128]{2,1,0:T(8,128)}, bf16[16,1024,1024]{2,1,0:T(8,128)(2,1)}) custom-call(f32[16,1024]{1,0:T(8,128)} %multiply_multiply_fusion.pts_ref, bf16[128,1024]{1,0:T(8,128)(2,1)} %fusion.signs_ref), custom_call_target="tpu_custom_call" | custom-call | tf_op jit(solution)/shard_map/lanczos/pallas_call | solution.py:356
  227.8 2.8 %multiply_add_fusion = (f32[128]{0:T(128)}, f32[128]{0:T(128)}) fusion(f32[3,8,128]{2,1,0:T(8,128)} %get-tuple-element.3), kind=kLoop, calls=%fused_computation.16 | loop fusion | flops 99968 | bytes 4096 | tf_op jit(solution)/shard_map/add | solution.py:339

commit v2 on v1

--- a/solution.py
+++ b/solution.py
@@ -154,10 +154,9 @@
     vecs[0] = signs_ref[...]
     direction[...] = signs_ref[...].astype(jnp.float32)
     right[...] = features(pts_ref[...], False).astype(jnp.bfloat16)
-    for k in range(1, blocks):
-        arrived(*pts, k)
-
-    def poll(pack, pair):
+    arrived(vecs, signs_ref, vec_recv, vec_send, 0)
+
+    def poll(packs, pair, begun):
         group = max(half // 4, 1)
         for g in range(0, half, group):
             @pl.when((pair >= g) & (pair < g + group))
@@ -166,7 +165,9 @@
                     @pl.when(pair == t)
                     def _():
                         for k in (2 * t, 2 * t + 1):
-                            arrived(*pack, k)
+                            for pack in packs:
+                                if k or not begun:
+                                    arrived(*pack, k)
 
     def form(k, chunk):
         left[...] = features(points[k], True).T.astype(jnp.bfloat16)
@@ -232,7 +233,7 @@
         pack = (vecs, signs_ref if step == 0 else vecs.at[0], vec_recv, vec_send)
         if step == 0:
             def first(pair, carry):
-                poll(pack, pair)
+                poll((pts, pack), pair, True)
                 slot = lax.rem(pair, 2)
                 form(2 * pair, near.at[pair])
                 apply(2 * pair, near.at[pair])
@@ -251,7 +252,7 @@
                 write(pair % 2, pair).wait()
         else:
             def later(pair, carry):
-                poll(pack, pair)
+                poll((pack,), pair, False)
                 slot = lax.rem(pair, 2)
 
                 @pl.when(pair + 1 < half)

time: 231 us -> 214 us (0.926)
  Pallas kernels: 224 us -> 207 us
    pallas_call x1, Pallas kernels: 224 us -> 207 us  [per_device(): pl.pallas_call(functools.partial(kernel, rows, cols, order, children), ou...]
where the time goes in v2:
time: 214 us
  Pallas kernels  207 us (97%)
  other arithmetic  5.13 us (2%)
    pallas_call x1, Pallas kernels, per_device(): pl.pallas_call(functools.partial(kernel, rows, cols, order, children), ou...  207 us

profile of v2, /device:TPU:0, one launch (start us, length us, event | category | flops | bytes accessed | tf_op | source)
XLA Modules:
  0.0 213.9 jit_solution(16903427718996437295)
XLA Ops:
  0.6 1.5 multiply_multiply_fusion.pts_ref
  2.2 1.2 copy.5
  3.4 0.8 fusion.signs_ref
  4.2 206.9 %lanczos.1 = (f32[3,8,128]{2,1,0:T(8,128)}, bf16[16,1024,1024]{2,1,0:T(8,128)(2,1)}) custom-call(f32[16,1024]{1,0:T(8,128)} %multiply_multiply_fusion.pts_ref, bf16[128,1024]{1,0:T(8,128)(2,1)} %fusion.signs_ref), custom_call_target="tpu_custom_call" | custom-call | tf_op jit(solution)/shard_map/lanczos/pallas_call | solution.py:357
  211.1 2.8 %multiply_add_fusion = (f32[128]{0:T(128)}, f32[128]{0:T(128)}) fusion(f32[3,8,128]{2,1,0:T(8,128)} %get-tuple-element.3), kind=kLoop, calls=%fused_computation.16 | loop fusion | flops 99968 | bytes 4096 | tf_op jit(solution)/shard_map/add | solution.py:340
